TPU v7x, 128 devices: a whole 4x4x4 slice. The times are simulated.
128 devices in a mesh: task: 8 (over x_hi, y), tp: 16 (over z, x_lo, core).
Axes of the slice: x: 4 (x_hi: 2, x_lo: 2; x = x_hi * 2 + x_lo), y: 4, z: 4, core: 2. Of those that a mesh axis runs over, the one named last changes fastest.
Arguments:
- observations: bfloat16 [256, 16, 4096], P('task', None, 'tp'), may hold values from -6 to 6
- gain: float32 [4096], P('tp'), may hold values from 0.5 to 1.5
- w_in: bfloat16 [4096, 4096], P(None, 'tp'), may hold values from -0.09375 to 0.09375
- w_mix: bfloat16 [4096, 4096], P('tp'), may hold values from -0.09375 to 0.09375
- w_out: bfloat16 [4096, 4096], P(None, 'tp'), may hold values from -0.09375 to 0.09375
- w_head: bfloat16 [4096, 75], P('tp'), may hold values from -0.09375 to 0.09375
- head_bias: float32 [75], replicated, may hold values from -4 to 4
- pop_mean: float32 [57], replicated, may hold values from -8 to 8
- pop_scale: float32 [57], replicated, may hold values from 0.5 to 4
- task_indices: int32 [256], P('task'), may hold values from 0 to 56
- actions: int32 [256, 15], P('task'), may hold values from 0 to 17
- rewards: float32 [256, 15], P('task'), may hold values from -18 to 27
- episode_ends: int32 [256, 15], P('task'), may hold values 0 or 1
- behaviour_log_prob: float32 [256, 15], P('task'), may hold values from -4.5 to -1.5
Outputs:
- grad_w_in: float32 [4096, 4096], P(None, 'tp')
- grad_w_mix: float32 [4096, 4096], P('tp')
- grad_w_out: float32 [4096, 4096], P(None, 'tp')
- grad_gain: float32 [4096], P('tp')
- grad_head: float32 [4096, 75], P('tp')
- grad_head_bias: float32 [75], replicated
- new_head: bfloat16 [4096, 75], P('tp')
- new_bias: float32 [75], replicated
- updated_return_mean: float32 [57], replicated
- updated_return_scale: float32 [57], replicated
All inputs are finite; a program needn't handle non-finite values. No bound on the sum of `episode_ends` on one device may be relied on, other than what follows from the above.
Results may differ from a plain program's by a relative error of at most 0.03.
Values may be sent and summed in bfloat16 or wider, within the bound.
A program may use at most 128 MiB of HBM per device.

v0:
```python
import jax
import jax.numpy as jnp
from jax import lax
from jax.sharding import PartitionSpec as P

ACTIONS = 18
TASKS = 57
DISCOUNT = 0.99
BASELINE_COST = 0.5
ENTROPY_COST = 0.01
POPART_PRIOR = 64.0
NORM_EPS = 1e-06


def sent_to_all(value, axis):
    copies = jnp.broadcast_to(value, (lax.axis_size(axis), *value.shape))
    return lax.all_to_all(copies, axis, split_axis=0, concat_axis=0, tiled=True)


def of_everyone(value, axis):
    everything = sent_to_all(value, axis)
    return jnp.sum(everything, axis=0)


def packed_total(arrays, axis):
    line, at, gathered = (jnp.concatenate([a.reshape(-1) for a in arrays]), 0, [])
    subtotal = of_everyone(line, axis)
    for a in arrays:
        gathered.append(subtotal[at : at + a.size].reshape(a.shape))
        at += a.size
    return tuple(gathered)


def cut_along(value, dim, devices):
    before, after = (value.shape[:dim], value.shape[dim + 1 :])
    return jnp.moveaxis(value.reshape(*before, devices, -1, *after), dim, 0)


def sum_at_owner(value, axis, dim):
    parts = cut_along(value, dim, lax.axis_size(axis))
    arrived = lax.all_to_all(parts, axis, split_axis=0, concat_axis=0, tiled=True)
    return arrived.astype(jnp.float32).sum(axis=0)


def joined_along(parts, dim):
    dims = list(parts.shape[1:])
    dims[dim] *= parts.shape[0]
    return jnp.moveaxis(parts, 0, dim).reshape(dims)


def gathered_copies(value, axis, dim):
    parts = sent_to_all(value, axis)
    return joined_along(parts, dim)


def summed_on_arrival(value, axis, dim):
    parts = cut_along(value, dim, lax.axis_size(axis))
    arrived = lax.all_to_all(parts, axis, split_axis=0, concat_axis=0, tiled=True)
    return arrived.sum(axis=0)


def silu_slope(before):
    sigmoid = jax.nn.sigmoid(before)
    return sigmoid * (1.0 + before * (1.0 - sigmoid))


def discounted_sums(values, factors):

    def advance(running, column):
        latest = column[0] + column[1] * running
        return (latest, latest)

    opening = jnp.zeros((values.shape[0],), jnp.float32)
    ending, stacked = lax.scan(advance, opening, (values.T, factors.T), reverse=True)
    return stacked.T


def task_onehot(task_indices):
    return (task_indices[:, None] == jnp.arange(TASKS, dtype=jnp.int32)[None, :]).astype(
        jnp.float32
    )


def popart_partials(task_indices, rewards, discount_factors):
    returns = discounted_sums(rewards, discount_factors)
    task_table = task_onehot(task_indices)
    counts = jnp.sum(task_table, axis=0) * rewards.shape[1]
    totals = jnp.dot(task_table.T, jnp.sum(returns, axis=1))
    squares = jnp.dot(task_table.T, jnp.sum(returns * returns, axis=1))
    return (counts, totals, squares)


def popart_update(counts, totals, squares, pop_mean, pop_scale):
    mixing = counts / (counts + POPART_PRIOR)
    safe_counts = jnp.maximum(counts, 1.0)
    batch_mean = totals / safe_counts
    batch_square = squares / safe_counts
    updated_return_mean = (1.0 - mixing) * pop_mean + mixing * batch_mean
    mean_gap = batch_mean - pop_mean
    variance = (
        (1.0 - mixing) * pop_scale * pop_scale
        + mixing * (batch_square - batch_mean * batch_mean)
        + mixing * (1.0 - mixing) * mean_gap * mean_gap
    )
    return (updated_return_mean, jnp.sqrt(variance))


def rescale_head(w_head, head_bias, pop_mean, pop_scale, updated_return_mean, updated_return_scale):
    scale_ratio = pop_scale / updated_return_scale
    column_scale = jnp.concatenate([jnp.ones((ACTIONS,), jnp.float32), scale_ratio])
    new_head = (w_head.astype(jnp.float32) * column_scale[None, :]).astype(jnp.bfloat16)
    value_bias = (
        pop_scale * head_bias[ACTIONS:] + pop_mean - updated_return_mean
    ) / updated_return_scale
    new_bias = jnp.concatenate([head_bias[:ACTIONS], value_bias])
    return (new_head, new_bias)


def importance_trace_loss(
    head_value_estimates,
    task_indices,
    actions,
    rewards,
    discount_factors,
    behaviour_log_prob,
    updated_return_mean,
    updated_return_scale,
    loss_weighting,
):
    task_table = task_onehot(task_indices)
    env_mean = jnp.dot(task_table, updated_return_mean)[:, None]
    env_scale = jnp.dot(task_table, updated_return_scale)[:, None]
    logits = head_value_estimates[:, :-1, :ACTIONS]
    norm_values = jnp.sum(head_value_estimates[:, :, ACTIONS:] * task_table[:, None, :], axis=2)
    values = lax.stop_gradient(norm_values * env_scale + env_mean)
    log_total = jnp.log(jnp.sum(jnp.exp(logits), axis=2))
    chosen = actions[:, :, None] == jnp.arange(ACTIONS, dtype=jnp.int32)[None, None, :]
    log_policy = jnp.sum(jnp.where(chosen, logits, 0.0), axis=2) - log_total
    clipped = jnp.minimum(jnp.exp(lax.stop_gradient(log_policy) - behaviour_log_prob), 1.0)
    deltas = clipped * (rewards + discount_factors * values[:, 1:] - values[:, :-1])
    targets = values[:, :-1] + discounted_sums(deltas, discount_factors * clipped)
    following = jnp.concatenate([targets[:, 1:], values[:, -1:]], axis=1)
    advantage = lax.stop_gradient(
        clipped
        * ((rewards + discount_factors * following - env_mean) / env_scale - norm_values[:, :-1])
    )
    normed_targets = lax.stop_gradient((targets - env_mean) / env_scale)
    policy = jnp.exp(logits - log_total[:, :, None])
    entropy = -jnp.sum(policy * (logits - log_total[:, :, None]), axis=2)
    per_frame = (
        -advantage * log_policy
        + 0.5 * BASELINE_COST * (normed_targets - norm_values[:, :-1]) ** 2
        - ENTROPY_COST * entropy
    )
    return loss_weighting * jnp.sum(per_frame)


def on_device(
    observations,
    gain,
    w_in,
    w_mix,
    w_out,
    w_head,
    head_bias,
    pop_mean,
    pop_scale,
    task_indices,
    actions,
    rewards,
    episode_ends,
    behaviour_log_prob,
):
    env_count, frames, part_width = observations.shape
    groups = lax.axis_size("tp")
    full_width = part_width * groups
    row_count = env_count * frames
    local_rows = row_count // groups
    own_tokens = observations.reshape(row_count, part_width)
    discount_factors = DISCOUNT * (1.0 - episode_ends.astype(jnp.float32))
    counts, totals, squares = popart_partials(task_indices, rewards, discount_factors)
    counts, totals, squares = packed_total((counts, totals, squares), "task")
    updated_return_mean, updated_return_scale = popart_update(
        counts, totals, squares, pop_mean, pop_scale
    )
    new_head, new_bias = rescale_head(
        w_head, head_bias, pop_mean, pop_scale, updated_return_mean, updated_return_scale
    )
    loss_weighting = float(env_count * lax.axis_size("task")) ** (-0.5)
    tokens, gain_all = (
        lax.all_gather(own_tokens, "tp", axis=1, tiled=True),
        lax.all_gather(gain.astype(jnp.bfloat16), "tp", axis=0, tiled=True).astype(gain.dtype),
    )
    row_offset = lax.axis_index("tp") * local_rows
    token_rows = lax.dynamic_slice_in_dim(tokens, row_offset, local_rows, 0)
    pre_in = jnp.dot(tokens, w_in, preferred_element_type=jnp.float32)
    hidden_in = jax.nn.silu(pre_in).astype(jnp.bfloat16)
    hidden_rows = hidden_in
    mix_sum = lax.psum_scatter(
        jnp.dot(hidden_rows, w_mix, preferred_element_type=jnp.float32).astype(jnp.bfloat16),
        "tp",
        scatter_dimension=0,
        tiled=True,
    ).astype(jnp.float32)
    residual = token_rows.astype(jnp.float32) + mix_sum
    inverse = lax.rsqrt(jnp.mean(residual * residual, axis=1, keepdims=True) + NORM_EPS)
    normed = (residual * inverse * gain_all[None, :]).astype(jnp.bfloat16)
    normed_all = lax.all_gather(normed, "tp", axis=0, tiled=True)
    pre_out = jnp.dot(normed_all, w_out, preferred_element_type=jnp.float32)
    hidden_out = jax.nn.silu(pre_out).astype(jnp.bfloat16)
    head_terms = jnp.dot(hidden_out, new_head, preferred_element_type=jnp.float32)
    env_share = env_count // groups
    env_offset = lax.axis_index("tp") * env_share

    def select_envs(source):
        return lax.dynamic_slice_in_dim(source, env_offset, env_share, 0)

    head_value_estimates = (
        sum_at_owner(head_terms.astype(jnp.bfloat16), "tp", 0) + new_bias[None, :]
    )
    head_value_estimates = head_value_estimates.reshape(env_share, frames, -1)

    def share_loss(network_outputs):
        return importance_trace_loss(
            network_outputs,
            select_envs(task_indices),
            select_envs(actions),
            select_envs(rewards),
            select_envs(discount_factors),
            select_envs(behaviour_log_prob),
            updated_return_mean,
            updated_return_scale,
            loss_weighting,
        )

    loss_value, pullback = jax.vjp(share_loss, head_value_estimates)
    (d_heads,) = pullback(jnp.ones((), jnp.float32))
    d_local = d_heads.reshape(env_share * frames, -1).astype(jnp.bfloat16)
    d_rounded = gathered_copies(d_local, "tp", 0)
    grad_head = jnp.dot(hidden_out.T, d_rounded, preferred_element_type=jnp.float32)
    grad_bias = jnp.sum(d_rounded.astype(jnp.float32), axis=0)
    d_hidden_out = jnp.dot(d_rounded, new_head.T, preferred_element_type=jnp.float32)
    d_pre_out = (d_hidden_out * silu_slope(pre_out)).astype(jnp.bfloat16)
    grad_out = jnp.dot(normed_all.T, d_pre_out, preferred_element_type=jnp.float32)
    d_normed = lax.psum_scatter(
        jnp.dot(d_pre_out, w_out.T, preferred_element_type=jnp.float32).astype(jnp.bfloat16),
        "tp",
        scatter_dimension=0,
        tiled=True,
    ).astype(jnp.float32)
    scaled = d_normed * gain_all[None, :]
    inner_sum = jnp.sum(scaled * residual, axis=1, keepdims=True)
    d_residual = (inverse * scaled - residual * inverse**3 * inner_sum / full_width).astype(
        jnp.bfloat16
    )
    grad_gain = summed_on_arrival(jnp.sum(d_normed * residual * inverse, axis=0), "tp", 0)
    arrived = lax.all_gather(d_residual, "tp", axis=0, tiled=True)
    hidden_rows = hidden_in
    grad_part = jnp.dot(hidden_rows.T, arrived, preferred_element_type=jnp.float32)
    d_hidden = jnp.dot(arrived, w_mix.T, preferred_element_type=jnp.float32)
    grad_mix = grad_part
    d_pre_in = (d_hidden * silu_slope(pre_in)).astype(jnp.bfloat16)
    grad_in = jnp.dot(tokens.T, d_pre_in, preferred_element_type=jnp.float32)
    grad_in, grad_mix, grad_out, grad_gain, grad_head, grad_bias = (
        lax.psum(grad_in.astype(jnp.bfloat16), "task").astype(jnp.float32),
        lax.psum(grad_mix.astype(jnp.bfloat16), "task").astype(jnp.float32),
        lax.psum(grad_out.astype(jnp.bfloat16), "task").astype(jnp.float32),
        lax.psum(grad_gain.astype(jnp.bfloat16), "task").astype(jnp.float32),
        lax.psum(grad_head.astype(jnp.bfloat16), "task").astype(jnp.float32),
        lax.psum(grad_bias.astype(jnp.bfloat16), "task").astype(jnp.float32),
    )
    return (
        grad_in,
        grad_mix,
        grad_out,
        grad_gain,
        grad_head,
        grad_bias,
        new_head,
        new_bias,
        updated_return_mean,
        updated_return_scale,
    )


def solution(mesh):
    in_specs = (
        P("task", None, "tp"),
        P("tp"),
        P(None, "tp"),
        P("tp", None),
        P(None, "tp"),
        P("tp", None),
        P(),
        P(),
        P(),
        P("task"),
        P("task", None),
        P("task", None),
        P("task", None),
        P("task", None),
    )
    out_specs = (
        P(None, "tp"),
        P("tp", None),
        P(None, "tp"),
        P("tp"),
        P("tp", None),
        P(),
        P("tp", None),
        P(),
        P(),
        P(),
    )
    return jax.shard_map(
        on_device, mesh=mesh, in_specs=in_specs, out_specs=out_specs, check_vma=False
    )
```

profile of v0, /device:TPU:1, one launch (start us, length us, event | category | flops | bytes accessed | tf_op | source)
XLA Modules:
  0.0 498.5 jit_solution(18199204609391938755)
XLA Ops:
  7.2 0.7 all-gather.5.cloned.1.call-update
  8.0 50.4 %all-gather.5.cloned.1.call-done = bf16[512,4096]{1,0:T(8,128)(2,1)} async-done(((bf16[512,256]{1,0:T(8,128)(2,1)}), bf16[512,4096]{1,0:T(8,128)(2,1)}) %all-gather.5.cloned.1.call-update) | async-done | bytes 4194320 | tf_op jit(solution)/shard_map/all_gather | solution.py:191
  58.4 4.1 fusion.46
  62.5 3.3 convolution_convert_fusion.1
  66.0 18.6 %all-gather = bf16[16,1,256]{2,1,0:T(2,128)(2,1)S(1)} all-gather(bf16[1,1,256]{2,1,0:T(2,128)(2,1)S(1)} %reshape.98), channel_id=1, replica_groups=mesh['task'=8,'tp'=16] {'tp'}, dimensions={0}, use_global_device_ids=true | all-gather | bytes 8704 | tf_op jit(solution)/shard_map/all_gather | solution.py:192
  84.6 49.5 %reduce-scatter.3.cloned.1.call-done = bf16[32,4096]{1,0:T(8,128)(2,1)} async-done(((bf16[512,4096]{1,0:T(8,128)(2,1)}), bf16[32,4096]{1,0:T(8,128)(2,1)}) %reduce-scatter.3.cloned.1.call-update) | async-done | bytes 262160 | tf_op jit(solution)/shard_map/reduce_scatter | solution.py:199
  134.1 1.2 multiply_reduce_fusion
  135.3 0.5 multiply_multiply_fusion.1
  135.8 1.8 multiply_convert_fusion.1
  137.9 1.1 while.34
  139.1 0.1 convolution_bitcast_fusion.3
  139.2 0.1 convolution_bitcast_fusion.2
  139.5 0.6 broadcast_in_dim.72
  140.1 6.2 %all-to-all-start = ((f32[8,1,171]{2,1,0:T(1,128)}), f32[8,1,171]{2,1,0:T(1,128)S(1)}, u32[]{:S(2)}, u32[]{:S(2)}) async-start(f32[8,1,171]{2,1,0:T(1,128)} %broadcast_in_dim.72), calls=%async_computation.1 | async-start | bytes 16384 | tf_op jit(solution)/shard_map/all_to_all | solution.py:17
  146.9 6.0 %all-to-all-done = f32[8,1,171]{2,1,0:T(1,128)S(1)} async-done(((f32[8,1,171]{2,1,0:T(1,128)}), f32[8,1,171]{2,1,0:T(1,128)S(1)}, u32[]{:S(2)}, u32[]{:S(2)}) %all-to-all-start) | async-done | bytes 5504 | tf_op jit(solution)/shard_map/all_to_all | solution.py:17
  153.1 0.2 convolution_bitcast_fusion.1
  153.3 0.2 convolution_bitcast_fusion
  153.6 23.3 %all-gather.7.cloned.1.call-done = bf16[512,4096]{1,0:T(8,128)(2,1)} async-done(((bf16[32,4096]{1,0:T(8,128)(2,1)}), bf16[512,4096]{1,0:T(8,128)(2,1)}) %all-gather.7.cloned.1.call-update) | async-done | bytes 4194320 | tf_op jit(solution)/shard_map/all_gather | solution.py:208
  176.8 4.9 multiply_convert_fusion
  181.8 0.2 convolution_convert_fusion.5
  182.0 0.8 copy.88
  182.8 4.2 all-to-all-start.1
  187.0 6.0 %all-to-all-done.1 = bf16[16,32,75]{2,1,0:T(8,128)(2,1)S(1)} async-done(((bf16[16,32,75]{2,1,0:T(8,128)(2,1)}), bf16[16,32,75]{2,1,0:T(8,128)(2,1)S(1)}, u32[]{:S(2)}, u32[]{:S(2)}) %all-to-all-start.1) | async-done | bytes 76832 | tf_op jit(solution)/shard_map/all_to_all | solution.py:41
  193.2 0.2 fusion.19
  193.5 0.2 multiply_reduce_fusion.1
  194.0 1.1 while.35
  195.7 9.4 %all_to_all.25 = bf16[16,32,75]{2,1,0:T(8,128)(2,1)S(1)} all-to-all(bf16[16,32,75]{2,1,0:T(8,128)(2,1)S(1)} %broadcast_in_dim.79), channel_id=1, replica_groups=mesh['task'=8,'tp'=16] {'tp'}, dimensions={0} | all-to-all | bytes 153600 | tf_op jit(solution)/shard_map/all_to_all | solution.py:17
  205.1 1.3 fusion.5
  206.4 3.3 convolution_convert_fusion
  209.8 67.0 %reduce-scatter.5.cloned.1.call-done = bf16[32,4096]{1,0:T(8,128)(2,1)} async-done(((bf16[512,4096]{1,0:T(8,128)(2,1)}), bf16[32,4096]{1,0:T(8,128)(2,1)}) %reduce-scatter.5.cloned.1.call-update) | async-done | bytes 262160 | tf_op jit(solution)/shard_map/reduce_scatter | solution.py:245
  276.8 1.8 fusion.13
  278.7 2.0 fusion.10
  280.6 0.2 all-reduce.8.cloned.1.call-start
  280.9 4.8 convolution_convert_fusion.2
  285.7 33.9 %all-gather.9.cloned.1.call-done = bf16[512,4096]{1,0:T(8,128)(2,1)} async-done(((bf16[32,4096]{1,0:T(8,128)(2,1)}), bf16[512,4096]{1,0:T(8,128)(2,1)}) %all-gather.9.cloned.1.call-update) | async-done | bytes 4194320 | tf_op jit(solution)/shard_map/all_gather | solution.py:257
  319.6 9.4 %fusion.4 = bf16[4096,256]{0,1:T(8,128)(2,1)} fusion(bf16[512,4096]{1,0:T(8,128)(2,1)} %all-gather.5.cloned.1.call-done, bf16[512,4096]{1,0:T(8,128)(2,1)} %all-gather.9.cloned.1.call-done, bf16[256,4096]{1,0:T(8,128)(2,1)S(1)} %copy-done, f32[512,256]{1,0:T(8,128)S(1)} %fusion.46), kind=kOutput, calls=%fused_computation.11 | convolution fusion | flops 2149711872 | bytes 13107200 | tf_op jit(solution)/shard_map/dot_general | solution.py:263
  329.0 4.8 convolution_convert_fusion.3
  333.8 4.4 all-to-all-start.3
  338.2 0.2 convolution_convert_fusion.6
  338.5 5.5 %all-to-all-done.3 = f32[16,1,256]{2,1,0:T(1,128)S(1)} async-done(((f32[16,1,256]{2,1,0:T(1,128)}), f32[16,1,256]{2,1,0:T(1,128)S(1)}, u32[]{:S(2)}, u32[]{:S(2)}) %all-to-all-start.3) | async-done | bytes 16416 | tf_op jit(solution)/shard_map/all_to_all | solution.py:58
  344.0 38.7 %all-reduce.4 = (bf16[256]{0:T(256)(128)(2,1)S(1)}, bf16[256,75]{0,1:T(8,128)(2,1)S(1)}, bf16[75]{0:T(256)(128)(2,1)S(1)}) all-reduce(bf16[256]{0:T(256)(128)(2,1)S(1)} %reduce_sum.162, bf16[256,75]{0,1:T(8,128)(2,1)S(1)} %convolution_convert_fusion.6, bf16[75]{0:T(256)(128)(2,1)S(1)} %reduce_sum.163), channel_id=1, replica_groups=mesh['task'=8,'tp'=16] {'task'}, use_global_device_ids=true, to_apply=%region_23.24 | all-reduce | flops 19531 | bytes 78124 | tf_op jit(solution)/shard_map/psum | solution.py:268
  382.7 0.6 convert_element_type.138
  383.3 0.5 convert_element_type.141
  383.8 0.6 convert_element_type.140
  384.4 96.4 %all-reduce.8.cloned.1.call-done = (bf16[4096,256]{0,1:T(8,128)(2,1)}, bf16[256,4096]{1,0:T(8,128)(2,1)}, bf16[4096,256]{1,0:T(8,128)(2,1)}) async-done(((bf16[4096,256]{0,1:T(8,128)(2,1)}, bf16[256,4096]{1,0:T(8,128)(2,1)}, bf16[4096,256]{1,0:T(8,128)(2,1)}), (bf16[4096,256]{0,1:T(8,128)(2,1)}, bf16[256,4096]{1,0:T(8,128)(2,1)}, bf16[4096,256]{1,0:T(8,128)(2,1)})) %all-reduce.8.cloned.1.call-update) | async-done | bytes 6291472 | tf_op jit(solution)/shard_map/psum | solution.py:265
  480.8 4.3 copy.105
  485.1 4.2 convert_element_type.134
  489.3 2.3 convert_element_type.136
  (156 shorter events, 4.7 us)
Async XLA Ops:
  7.2 55.3 %copy-start = (bf16[256,4096]{1,0:T(8,128)(2,1)S(1)}, bf16[256,4096]{1,0:T(8,128)(2,1)}, u32[]{:S(2)}) copy-start(bf16[256,4096]{1,0:T(8,128)(2,1)} %param.21) | copy-start | bytes 6291460
  7.2 51.2 %all-gather.5.cloned.1.call-start = ((), (), s32[]{:S(2)}) async-start(), calls=%async_computation.6 | async-start | bytes 4456448 | tf_op jit(solution)/shard_map/all_gather | solution.py:191
  7.9 126.2 %reduce-scatter.3.cloned.1.call-start = ((), (), s32[]{:S(2)}) async-start(), calls=%async_computation.7 | async-start | bytes 4456448 | tf_op jit(solution)/shard_map/reduce_scatter | solution.py:199
  62.5 3.5 copy-start.17
  65.8 71.9 %copy-start.7 = (s32[32,15]{0,1:T(8,128)S(1)}, s32[32,15]{0,1:T(8,128)}, u32[]{:S(2)}) copy-start(s32[32,15]{0,1:T(8,128)} %param.30) | copy-start | bytes 5764
  65.8 72.1 %copy-start.6 = (f32[32,15]{0,1:T(8,128)S(1)}, f32[32,15]{0,1:T(8,128)}, u32[]{:S(2)}) copy-start(f32[32,15]{0,1:T(8,128)} %param.29) | copy-start | bytes 5764
  65.8 73.3 %copy-start.18 = (s32[32]{0:T(128)S(1)}, s32[32]{0:T(128)}, u32[]{:S(2)}) copy-start(s32[32]{0:T(128)} %param.27) | copy-start | bytes 388
  65.8 80.6 %copy-start.9 = (f32[32,15]{0,1:T(8,128)S(1)}, f32[32,15]{0,1:T(8,128)}, u32[]{:S(2)}) copy-start(f32[32,15]{0,1:T(8,128)} %param.31) | copy-start | bytes 5764
  65.8 80.7 %copy-start.8 = (s32[32,15]{0,1:T(8,128)S(1)}, s32[32,15]{0,1:T(8,128)}, u32[]{:S(2)}) copy-start(s32[32,15]{0,1:T(8,128)} %param.28) | copy-start | bytes 5764
  65.8 87.1 %copy-start.12 = (f32[57]{0:T(128)S(1)}, f32[57]{0:T(128)}, u32[]{:S(2)}) copy-start(f32[57]{0:T(128)} %param.25) | copy-start | bytes 688
  65.8 87.1 %copy-start.13 = (f32[57]{0:T(128)S(1)}, f32[57]{0:T(128)}, u32[]{:S(2)}) copy-start(f32[57]{0:T(128)} %param.26) | copy-start | bytes 688
  65.8 87.0 %copy-start.14 = (f32[75]{0:T(128)S(1)}, f32[75]{0:T(128)}, u32[]{:S(2)}) copy-start(f32[75]{0:T(128)} %param.24) | copy-start | bytes 904
  65.9 87.6 %copy-start.5 = (bf16[256,75]{0,1:T(8,128)(2,1)S(1)}, bf16[256,75]{0,1:T(8,128)(2,1)}, u32[]{:S(2)}) copy-start(bf16[256,75]{0,1:T(8,128)(2,1)} %param.23) | copy-start | bytes 115204
  65.9 111.0 %all-gather.7.cloned.1.call-start = ((), (), s32[]{:S(2)}) async-start(), calls=%async_computation.8 | async-start | bytes 4456448 | tf_op jit(solution)/shard_map/all_gather | solution.py:208
  135.8 1.9 copy-start.10
  140.1 12.7 %all-to-all-start = ((f32[8,1,171]{2,1,0:T(1,128)}), f32[8,1,171]{2,1,0:T(1,128)S(1)}, u32[]{:S(2)}, u32[]{:S(2)}) async-start(f32[8,1,171]{2,1,0:T(1,128)} %broadcast_in_dim.72), calls=%async_computation.1 | async-start | bytes 16384 | tf_op jit(solution)/shard_map/all_to_all | solution.py:17
  153.0 28.8 %copy-start.15 = (f32[57]{0:T(128)}, f32[57]{0:T(128)S(1)}, u32[]{:S(2)}) copy-start(f32[57]{0:T(128)S(1)} %get-tuple-element.394) | copy-start | bytes 688
  153.0 28.8 %copy-start.16 = (f32[57]{0:T(128)}, f32[57]{0:T(128)S(1)}, u32[]{:S(2)}) copy-start(f32[57]{0:T(128)S(1)} %get-tuple-element.395) | copy-start | bytes 688
  153.6 51.5 %copy-start.4 = (bf16[256,75]{0,1:T(8,128)(2,1)}, bf16[256,75]{0,1:T(8,128)(2,1)S(1)}, u32[]{:S(2)}) copy-start(bf16[256,75]{0,1:T(8,128)(2,1)S(1)} %multiply_convert_fusion.3) | copy-start | bytes 115204
  182.8 10.3 %all-to-all-start.1 = ((bf16[16,32,75]{2,1,0:T(8,128)(2,1)}), bf16[16,32,75]{2,1,0:T(8,128)(2,1)S(1)}, u32[]{:S(2)}, u32[]{:S(2)}) async-start(bf16[16,32,75]{2,1,0:T(8,128)(2,1)} %bitcast.8), calls=%async_computation.2 | async-start | bytes 262144 | tf_op jit(solution)/shard_map/all_to_all | solution.py:41
  186.9 89.9 %reduce-scatter.5.cloned.1.call-start = ((), (), s32[]{:S(2)}) async-start(), calls=%async_computation.9 | async-start | bytes 4456448 | tf_op jit(solution)/shard_map/reduce_scatter | solution.py:245
  187.0 6.0 %copy-start.11 = (f32[75]{0:T(128)}, f32[75]{0:T(128)S(1)}, u32[]{:S(2)}) copy-start(f32[75]{0:T(128)S(1)} %pad_maximum_fusion.1) | copy-start | bytes 904
  195.2 11.2 %copy-start.3 = (bf16[4096,256]{1,0:T(8,128)(2,1)S(1)}, bf16[4096,256]{1,0:T(8,128)(2,1)}, u32[]{:S(2)}) copy-start(bf16[4096,256]{1,0:T(8,128)(2,1)} %param.22) | copy-start | bytes 6291460
  209.7 67.1 %copy-start.1 = (bf16[32,4096]{1,0:T(8,128)(2,1)S(1)}, bf16[32,4096]{1,0:T(8,128)(2,1)}, u32[]{:S(2)}) copy-start(bf16[32,4096]{1,0:T(8,128)(2,1)} %reduce-scatter.3.cloned.1.call-done) | copy-start | bytes 786436
  209.7 109.8 %all-gather.9.cloned.1.call-start = ((), (), s32[]{:S(2)}) async-start(), calls=%async_computation.10 | async-start | bytes 4456448 | tf_op jit(solution)/shard_map/all_gather | solution.py:257
  280.6 200.2 %all-reduce.8.cloned.1.call-start = ((), (), s32[]{:S(2)}) async-start(), calls=%async_computation.11 | async-start | bytes 12582912 | tf_op jit(solution)/shard_map/psum | solution.py:265
  333.8 10.1 %all-to-all-start.3 = ((f32[16,1,256]{2,1,0:T(1,128)}), f32[16,1,256]{2,1,0:T(1,128)S(1)}, u32[]{:S(2)}, u32[]{:S(2)}) async-start(f32[16,1,256]{2,1,0:T(1,128)} %bitcast.20), calls=%async_computation.5 | async-start | bytes 32768 | tf_op jit(solution)/shard_map/all_to_all | solution.py:58
  485.1 4.3 copy-start.2
Sparse Core Ops, SparseCore 0:
  9.6 48.6 all-gather.4
  66.0 68.0 reduce-scatter.2
  137.8 38.9 all-gather.6
  209.9 66.9 reduce-scatter.4
  280.8 38.7 all-gather.8
  333.9 146.8 all-reduce.7
where the time goes:
time: 499 us
  waiting for transfers between devices  339 us (68%)
  blocking collectives  66.7 us (13%)
  matrix products  37 us (7%)
  other arithmetic  18 us (4%)
  starting transfers between devices  15.1 us (3%)
  between operations  14.4 us (3%)
  local copies, waits for them, and re-layouts  8.14 us (2%)
    psum x1, waiting for transfers between devices, on_device(): lax.psum(grad_in.astype(jnp.bfloat16), 'task').astype(jnp.float32)  96.4 us
    reduce_scatter x1, waiting for transfers between devices, on_device(): lax.psum_scatter(jnp.dot(d_pre_out, w_out.T, preferred_element_type=jnp.f...  67 us
    all_gather x1, waiting for transfers between devices, on_device(): lax.all_gather(own_tokens, 'tp', axis=1, tiled=True)  50.4 us
    reduce_scatter x1, waiting for transfers between devices, on_device(): lax.psum_scatter(jnp.dot(hidden_rows, w_mix, preferred_element_type=jnp.f...  49.5 us
    psum x1, blocking collectives, on_device(): lax.psum(grad_gain.astype(jnp.bfloat16), 'task').astype(jnp.float32)  38.7 us
    all_gather x1, waiting for transfers between devices, on_device(): arrived = lax.all_gather(d_residual, 'tp', axis=0, tiled=True)  33.9 us
    all_gather x1, waiting for transfers between devices, on_device(): normed_all = lax.all_gather(normed, 'tp', axis=0, tiled=True)  23.3 us
    all_gather x1, blocking collectives, on_device(): lax.all_gather(gain.astype(jnp.bfloat16), 'tp', axis=0, tiled=True)  18.6 us
  transfers between devices with their start and end apart: 9, of which 9 were waited for; matrix products, arithmetic and copies ran while one was open for 2% of the time, Pallas kernels for 0%

commit v1 on v0

--- a/solution.py
+++ b/solution.py
@@ -188,7 +188,7 @@
     )
     loss_weighting = float(env_count * lax.axis_size("task")) ** (-0.5)
     tokens, gain_all = (
-        lax.all_gather(own_tokens, "tp", axis=1, tiled=True),
+        jnp.concatenate(lax.all_gather(own_tokens, "tp"), axis=1),
         lax.all_gather(gain.astype(jnp.bfloat16), "tp", axis=0, tiled=True).astype(gain.dtype),
     )
     row_offset = lax.axis_index("tp") * local_rows

time: 499 us -> 493 us (0.988)
  waiting for transfers between devices: 339 us -> 331 us
    all_gather x1, waiting for transfers between devices: 50.4 us -> 42.7 us  [on_device(): lax.all_gather(own_tokens, 'tp')]
where the time goes in v1:
time: 493 us
  waiting for transfers between devices  331 us (67%)
  blocking collectives  66.3 us (13%)
  matrix products  34.2 us (7%)
  other arithmetic  18 us (4%)
  starting transfers between devices  15.2 us (3%)
  between operations  14.5 us (3%)
  local copies, waits for them, and re-layouts  13 us (3%)
    psum x1, waiting for transfers between devices, on_device(): lax.psum(grad_in.astype(jnp.bfloat16), 'task').astype(jnp.float32)  96.4 us
    reduce_scatter x1, waiting for transfers between devices, on_device(): lax.psum_scatter(jnp.dot(d_pre_out, w_out.T, preferred_element_type=jnp.f...  66.8 us
    reduce_scatter x1, waiting for transfers between devices, on_device(): lax.psum_scatter(jnp.dot(hidden_rows, w_mix, preferred_element_type=jnp.f...  49.8 us
    all_gather x1, waiting for transfers between devices, on_device(): lax.all_gather(own_tokens, 'tp')  42.7 us
    psum x1, blocking collectives, on_device(): lax.psum(grad_gain.astype(jnp.bfloat16), 'task').astype(jnp.float32)  38.7 us
    all_gather x1, waiting for transfers between devices, on_device(): arrived = lax.all_gather(d_residual, 'tp', axis=0, tiled=True)  34 us
    all_gather x1, waiting for transfers between devices, on_device(): normed_all = lax.all_gather(normed, 'tp', axis=0, tiled=True)  23.1 us
    all_gather x1, blocking collectives, on_device(): lax.all_gather(gain.astype(jnp.bfloat16), 'tp', axis=0, tiled=True)  18.2 us
  transfers between devices with their start and end apart: 9, of which 9 were waited for; matrix products, arithmetic and copies ran while one was open for 2% of the time, Pallas kernels for 0%

profile of v1, /device:TPU:1, one launch (start us, length us, event | category | flops | bytes accessed | tf_op | source)
XLA Modules:
  0.0 492.7 jit_solution(17312258095836179197)
XLA Ops:
  7.2 0.7 all-gather.5.cloned.1.call-update
  8.0 42.7 %all-gather.5.cloned.1.call-done = bf16[16,512,256]{2,1,0:T(8,128)(2,1)} async-done(((bf16[1,512,256]{2,1,0:T(8,128)(2,1)}), bf16[16,512,256]{2,1,0:T(8,128)(2,1)}) %all-gather.5.cloned.1.call-update) | async-done | bytes 4194320 | tf_op jit(solution)/shard_map/all_gather | solution.py:191
  50.7 2.9 copy.123
  53.6 2.0 copy-done.1
  55.6 1.2 fusion.46
  56.8 3.3 convolution_convert_fusion.1
  60.3 18.2 %all-gather = bf16[16,1,256]{2,1,0:T(2,128)(2,1)S(1)} all-gather(bf16[1,1,256]{2,1,0:T(2,128)(2,1)S(1)} %reshape.102), channel_id=1, replica_groups=mesh['task'=8,'tp'=16] {'tp'}, dimensions={0}, use_global_device_ids=true | all-gather | bytes 8704 | tf_op jit(solution)/shard_map/all_gather | solution.py:192
  78.6 49.8 %reduce-scatter.3.cloned.1.call-done = bf16[32,4096]{1,0:T(8,128)(2,1)} async-done(((bf16[512,4096]{1,0:T(8,128)(2,1)}), bf16[32,4096]{1,0:T(8,128)(2,1)}) %reduce-scatter.3.cloned.1.call-update) | async-done | bytes 262160 | tf_op jit(solution)/shard_map/reduce_scatter | solution.py:199
  128.4 1.2 multiply_reduce_fusion
  129.6 0.5 multiply_multiply_fusion.1
  130.1 1.8 multiply_convert_fusion.1
  132.2 1.1 while.34
  133.8 0.6 broadcast_in_dim.72
  134.4 6.1 %all-to-all-start = ((f32[8,1,171]{2,1,0:T(1,128)}), f32[8,1,171]{2,1,0:T(1,128)S(1)}, u32[]{:S(2)}, u32[]{:S(2)}) async-start(f32[8,1,171]{2,1,0:T(1,128)} %broadcast_in_dim.72), calls=%async_computation.1 | async-start | bytes 16384 | tf_op jit(solution)/shard_map/all_to_all | solution.py:17
  141.1 6.0 %all-to-all-done = f32[8,1,171]{2,1,0:T(1,128)S(1)} async-done(((f32[8,1,171]{2,1,0:T(1,128)}), f32[8,1,171]{2,1,0:T(1,128)S(1)}, u32[]{:S(2)}, u32[]{:S(2)}) %all-to-all-start) | async-done | bytes 5504 | tf_op jit(solution)/shard_map/all_to_all | solution.py:17
  147.4 0.2 convolution_bitcast_fusion.1
  147.5 0.2 convolution_bitcast_fusion
  147.8 23.1 %all-gather.7.cloned.1.call-done = bf16[512,4096]{1,0:T(8,128)(2,1)} async-done(((bf16[32,4096]{1,0:T(8,128)(2,1)}), bf16[512,4096]{1,0:T(8,128)(2,1)}) %all-gather.7.cloned.1.call-update) | async-done | bytes 4194320 | tf_op jit(solution)/shard_map/all_gather | solution.py:208
  171.0 4.9 multiply_convert_fusion
  175.9 0.2 convolution_convert_fusion.5
  176.1 0.8 copy.94
  176.9 4.3 all-to-all-start.1
  181.3 6.0 %all-to-all-done.1 = bf16[16,32,75]{2,1,0:T(8,128)(2,1)S(1)} async-done(((bf16[16,32,75]{2,1,0:T(8,128)(2,1)}), bf16[16,32,75]{2,1,0:T(8,128)(2,1)S(1)}, u32[]{:S(2)}, u32[]{:S(2)}) %all-to-all-start.1) | async-done | bytes 76832 | tf_op jit(solution)/shard_map/all_to_all | solution.py:41
  187.4 0.2 fusion.19
  187.7 0.2 multiply_reduce_fusion.1
  188.2 1.1 while.35
  189.9 9.4 %all_to_all.25 = bf16[16,32,75]{2,1,0:T(8,128)(2,1)S(1)} all-to-all(bf16[16,32,75]{2,1,0:T(8,128)(2,1)S(1)} %broadcast_in_dim.79), channel_id=1, replica_groups=mesh['task'=8,'tp'=16] {'tp'}, dimensions={0} | all-to-all | bytes 153600 | tf_op jit(solution)/shard_map/all_to_all | solution.py:17
  199.3 1.3 fusion.5
  200.6 3.3 convolution_convert_fusion
  204.0 66.8 %reduce-scatter.5.cloned.1.call-done = bf16[32,4096]{1,0:T(8,128)(2,1)} async-done(((bf16[512,4096]{1,0:T(8,128)(2,1)}), bf16[32,4096]{1,0:T(8,128)(2,1)}) %reduce-scatter.5.cloned.1.call-update) | async-done | bytes 262160 | tf_op jit(solution)/shard_map/reduce_scatter | solution.py:245
  270.9 1.8 fusion.13
  272.7 1.9 fusion.10
  274.7 0.2 all-reduce.8.cloned.1.call-start
  274.9 4.8 convolution_convert_fusion.2
  279.7 34.0 %all-gather.9.cloned.1.call-done = bf16[512,4096]{1,0:T(8,128)(2,1)} async-done(((bf16[32,4096]{1,0:T(8,128)(2,1)}), bf16[512,4096]{1,0:T(8,128)(2,1)}) %all-gather.9.cloned.1.call-update) | async-done | bytes 4194320 | tf_op jit(solution)/shard_map/all_gather | solution.py:257
  313.7 9.4 %fusion.4 = bf16[4096,256]{0,1:T(8,128)(2,1)} fusion(bf16[512,4096]{1,0:T(8,128)(2,1)} %bitcast.107, bf16[512,4096]{1,0:T(8,128)(2,1)} %all-gather.9.cloned.1.call-done, bf16[256,4096]{1,0:T(8,128)(2,1)S(1)} %copy-done, f32[512,256]{1,0:T(8,128)S(1)} %fusion.46), kind=kOutput, calls=%fused_computation.11 | convolution fusion | flops 2149711872 | bytes 13107200 | tf_op jit(solution)/shard_map/dot_general | solution.py:263
  323.1 4.8 convolution_convert_fusion.3
  328.0 4.4 all-to-all-start.3
  332.3 0.2 convolution_convert_fusion.6
  332.6 5.5 %all-to-all-done.3 = f32[16,1,256]{2,1,0:T(1,128)S(1)} async-done(((f32[16,1,256]{2,1,0:T(1,128)}), f32[16,1,256]{2,1,0:T(1,128)S(1)}, u32[]{:S(2)}, u32[]{:S(2)}) %all-to-all-start.3) | async-done | bytes 16416 | tf_op jit(solution)/shard_map/all_to_all | solution.py:58
  338.2 38.7 %all-reduce.4 = (bf16[256]{0:T(256)(128)(2,1)S(1)}, bf16[256,75]{0,1:T(8,128)(2,1)S(1)}, bf16[75]{0:T(256)(128)(2,1)S(1)}) all-reduce(bf16[256]{0:T(256)(128)(2,1)S(1)} %reduce_sum.162, bf16[256,75]{0,1:T(8,128)(2,1)S(1)} %convolution_convert_fusion.6, bf16[75]{0:T(256)(128)(2,1)S(1)} %reduce_sum.163), channel_id=1, replica_groups=mesh['task'=8,'tp'=16] {'task'}, use_global_device_ids=true, to_apply=%region_23.24 | all-reduce | flops 19531 | bytes 78124 | tf_op jit(solution)/shard_map/psum | solution.py:268
  376.9 0.6 convert_element_type.138
  377.4 0.5 convert_element_type.141
  377.9 0.6 convert_element_type.140
  378.6 96.4 %all-reduce.8.cloned.1.call-done = (bf16[4096,256]{0,1:T(8,128)(2,1)}, bf16[256,4096]{1,0:T(8,128)(2,1)}, bf16[4096,256]{1,0:T(8,128)(2,1)}) async-done(((bf16[4096,256]{0,1:T(8,128)(2,1)}, bf16[256,4096]{1,0:T(8,128)(2,1)}, bf16[4096,256]{1,0:T(8,128)(2,1)}), (bf16[4096,256]{0,1:T(8,128)(2,1)}, bf16[256,4096]{1,0:T(8,128)(2,1)}, bf16[4096,256]{1,0:T(8,128)(2,1)})) %all-reduce.8.cloned.1.call-update) | async-done | bytes 6291472 | tf_op jit(solution)/shard_map/psum | solution.py:265
  475.0 4.3 copy.111
  479.2 4.2 convert_element_type.134
  483.5 2.3 convert_element_type.136
  (161 shorter events, 5.0 us)
Async XLA Ops:
  7.2 49.7 %copy-start = (bf16[256,4096]{1,0:T(8,128)(2,1)S(1)}, bf16[256,4096]{1,0:T(8,128)(2,1)}, u32[]{:S(2)}) copy-start(bf16[256,4096]{1,0:T(8,128)(2,1)} %param.21) | copy-start | bytes 6291460
  7.2 43.5 %all-gather.5.cloned.1.call-start = ((), (), s32[]{:S(2)}) async-start(), calls=%async_computation.6 | async-start | bytes 4456448 | tf_op jit(solution)/shard_map/all_gather | solution.py:191
  7.9 120.4 %reduce-scatter.3.cloned.1.call-start = ((), (), s32[]{:S(2)}) async-start(), calls=%async_computation.7 | async-start | bytes 4456448 | tf_op jit(solution)/shard_map/reduce_scatter | solution.py:199
  50.7 4.9 copy-start.18
  53.5 2.0 copy-start.1
  56.8 3.5 copy-start.19
  60.1 71.9 %copy-start.8 = (s32[32,15]{0,1:T(8,128)S(1)}, s32[32,15]{0,1:T(8,128)}, u32[]{:S(2)}) copy-start(s32[32,15]{0,1:T(8,128)} %param.30) | copy-start | bytes 5764
  60.2 72.0 %copy-start.7 = (f32[32,15]{0,1:T(8,128)S(1)}, f32[32,15]{0,1:T(8,128)}, u32[]{:S(2)}) copy-start(f32[32,15]{0,1:T(8,128)} %param.29) | copy-start | bytes 5764
  60.2 73.2 %copy-start.20 = (s32[32]{0:T(128)S(1)}, s32[32]{0:T(128)}, u32[]{:S(2)}) copy-start(s32[32]{0:T(128)} %param.27) | copy-start | bytes 388
  60.2 80.5 %copy-start.10 = (f32[32,15]{0,1:T(8,128)S(1)}, f32[32,15]{0,1:T(8,128)}, u32[]{:S(2)}) copy-start(f32[32,15]{0,1:T(8,128)} %param.31) | copy-start | bytes 5764
  60.2 80.6 %copy-start.9 = (s32[32,15]{0,1:T(8,128)S(1)}, s32[32,15]{0,1:T(8,128)}, u32[]{:S(2)}) copy-start(s32[32,15]{0,1:T(8,128)} %param.28) | copy-start | bytes 5764
  60.2 87.0 %copy-start.13 = (f32[57]{0:T(128)S(1)}, f32[57]{0:T(128)}, u32[]{:S(2)}) copy-start(f32[57]{0:T(128)} %param.25) | copy-start | bytes 688
  60.2 87.0 %copy-start.14 = (f32[57]{0:T(128)S(1)}, f32[57]{0:T(128)}, u32[]{:S(2)}) copy-start(f32[57]{0:T(128)} %param.26) | copy-start | bytes 688
  60.2 87.0 %copy-start.15 = (f32[75]{0:T(128)S(1)}, f32[75]{0:T(128)}, u32[]{:S(2)}) copy-start(f32[75]{0:T(128)} %param.24) | copy-start | bytes 904
  60.2 87.5 %copy-start.6 = (bf16[256,75]{0,1:T(8,128)(2,1)S(1)}, bf16[256,75]{0,1:T(8,128)(2,1)}, u32[]{:S(2)}) copy-start(bf16[256,75]{0,1:T(8,128)(2,1)} %param.23) | copy-start | bytes 115204
  60.2 110.7 %all-gather.7.cloned.1.call-start = ((), (), s32[]{:S(2)}) async-start(), calls=%async_computation.8 | async-start | bytes 4456448 | tf_op jit(solution)/shard_map/all_gather | solution.py:208
  130.1 1.9 copy-start.11
  134.4 12.7 %all-to-all-start = ((f32[8,1,171]{2,1,0:T(1,128)}), f32[8,1,171]{2,1,0:T(1,128)S(1)}, u32[]{:S(2)}, u32[]{:S(2)}) async-start(f32[8,1,171]{2,1,0:T(1,128)} %broadcast_in_dim.72), calls=%async_computation.1 | async-start | bytes 16384 | tf_op jit(solution)/shard_map/all_to_all | solution.py:17
  147.2 28.7 %copy-start.16 = (f32[57]{0:T(128)}, f32[57]{0:T(128)S(1)}, u32[]{:S(2)}) copy-start(f32[57]{0:T(128)S(1)} %get-tuple-element.394) | copy-start | bytes 688
  147.3 28.6 %copy-start.17 = (f32[57]{0:T(128)}, f32[57]{0:T(128)S(1)}, u32[]{:S(2)}) copy-start(f32[57]{0:T(128)S(1)} %get-tuple-element.395) | copy-start | bytes 688
  147.8 51.5 %copy-start.5 = (bf16[256,75]{0,1:T(8,128)(2,1)}, bf16[256,75]{0,1:T(8,128)(2,1)S(1)}, u32[]{:S(2)}) copy-start(bf16[256,75]{0,1:T(8,128)(2,1)S(1)} %multiply_convert_fusion.3) | copy-start | bytes 115204
  176.9 10.4 %all-to-all-start.1 = ((bf16[16,32,75]{2,1,0:T(8,128)(2,1)}), bf16[16,32,75]{2,1,0:T(8,128)(2,1)S(1)}, u32[]{:S(2)}, u32[]{:S(2)}) async-start(bf16[16,32,75]{2,1,0:T(8,128)(2,1)} %bitcast.9), calls=%async_computation.2 | async-start | bytes 262144 | tf_op jit(solution)/shard_map/all_to_all | solution.py:41
  181.2 89.7 %reduce-scatter.5.cloned.1.call-start = ((), (), s32[]{:S(2)}) async-start(), calls=%async_computation.9 | async-start | bytes 4456448 | tf_op jit(solution)/shard_map/reduce_scatter | solution.py:245
  181.3 6.0 %copy-start.12 = (f32[75]{0:T(128)}, f32[75]{0:T(128)S(1)}, u32[]{:S(2)}) copy-start(f32[75]{0:T(128)S(1)} %pad_maximum_fusion.1) | copy-start | bytes 904
  189.4 11.2 %copy-start.4 = (bf16[4096,256]{1,0:T(8,128)(2,1)S(1)}, bf16[4096,256]{1,0:T(8,128)(2,1)}, u32[]{:S(2)}) copy-start(bf16[4096,256]{1,0:T(8,128)(2,1)} %param.22) | copy-start | bytes 6291460
  203.9 66.9 %copy-start.2 = (bf16[32,4096]{1,0:T(8,128)(2,1)S(1)}, bf16[32,4096]{1,0:T(8,128)(2,1)}, u32[]{:S(2)}) copy-start(bf16[32,4096]{1,0:T(8,128)(2,1)} %reduce-scatter.3.cloned.1.call-done) | copy-start | bytes 786436
  204.0 109.8 %all-gather.9.cloned.1.call-start = ((), (), s32[]{:S(2)}) async-start(), calls=%async_computation.10 | async-start | bytes 4456448 | tf_op jit(solution)/shard_map/all_gather | solution.py:257
  274.7 200.3 %all-reduce.8.cloned.1.call-start = ((), (), s32[]{:S(2)}) async-start(), calls=%async_computation.11 | async-start | bytes 12582912 | tf_op jit(solution)/shard_map/psum | solution.py:265
  328.0 10.1 %all-to-all-start.3 = ((f32[16,1,256]{2,1,0:T(1,128)}), f32[16,1,256]{2,1,0:T(1,128)S(1)}, u32[]{:S(2)}, u32[]{:S(2)}) async-start(f32[16,1,256]{2,1,0:T(1,128)} %bitcast.21), calls=%async_computation.5 | async-start | bytes 32768 | tf_op jit(solution)/shard_map/all_to_all | solution.py:58
  479.2 4.3 copy-start.3
Sparse Core Ops, SparseCore 0:
  9.7 40.9 all-gather.4
  60.4 67.9 reduce-scatter.2
  132.1 38.8 all-gather.6
  204.1 66.7 reduce-scatter.4
  274.8 38.9 all-gather.8
  328.1 146.8 all-reduce.7
